TPU v7x, 32 devices: a whole 2x2x4 slice. The times are simulated.
32 devices in a mesh: dp: 2 (over x), seq: 16 (over z, y, core).
Axes of the slice: x: 2, y: 2, z: 4, core: 2. Of those that a mesh axis runs over, the one named last changes fastest.
Arguments:
- tiles: bfloat16 [2, 16, 32, 4, 1024], P('dp', None, 'seq'), may hold values from -6 to 6
- patch_index: int32 [2, 16, 32, 4], P('dp', None, 'seq'), may hold values from 0 to 127
- pos_table: bfloat16 [128, 1024], replicated, may hold values from -6 to 6
- depth_kernel: bfloat16 [2, 27, 1024], replicated, may hold values from -1.25 to 1.25
- enc_gain: bfloat16 [2, 1024], replicated, may hold values from 0.099609375 to 1.8984375
- point_weight: bfloat16 [2, 1024, 1024], replicated, may hold values from -0.1875 to 0.1875
- action_ids: int32 [2, 16], replicated, may hold values from 0 to 7
- w_in: bfloat16 [1024, 5120], P('seq', 'dp'), may hold values from -0.1875 to 0.1875
- action_table: bfloat16 [8, 5120], P(None, 'dp'), may hold values from -6 to 6
- dyn_gain: bfloat16 [5120], P('dp'), may hold values from 0.099609375 to 1.8984375
- w_query: bfloat16 [5120, 5120], P('seq', 'dp'), may hold values from -0.078125 to 0.078125
- w_keyval: bfloat16 [5120, 2, 1024], P('seq', None, 'dp'), may hold values from -0.078125 to 0.078125
- seq_order: int32 [4], replicated, may hold values from 0 to 3, each once
Outputs:
- attended: bfloat16 [2, 16, 32, 4, 5120], P(None, None, 'seq', None, 'dp')
Inputs may be any that keep to these rules, and one draw needn't show every extreme that they name: `seq_order`: each of 0 to 3 appears once.
All inputs are finite; a program needn't handle non-finite values.
Results may differ from a plain program's by a relative error of at most 0.012.
Values may be sent and summed in bfloat16 or wider, within the bound.
A program may use at most 128 MiB of HBM per device.

v0:
```python
import jax
import jax.numpy as jnp
from jax import lax
from jax.sharding import PartitionSpec as P

DIM = 5120
HEAD = 128
Q_HEADS = 40
KV_HEADS = 8


def extended(block, sides, width):
    for axis, dim in sides:
        count = lax.axis_size(axis)
        forward = [(i, i + 1) for i in range(count - 1)]
        backward = [(target, source) for source, target in forward]
        low = lax.ppermute(
            lax.slice_in_dim(block, block.shape[dim] - width, None, axis=dim), axis, forward
        )
        high = lax.ppermute(lax.slice_in_dim(block, 0, width, axis=dim), axis, backward)
        block = jnp.concatenate([low, block, high], axis=dim)
    return block


def depth_block(padded, kernel, gains, weight):
    frames = padded.shape[1]
    height = padded.shape[2] - 2
    breadth = padded.shape[3]
    channels = padded.shape[4]
    framed = jnp.pad(padded.astype(jnp.float32), ((0, 0), (2, 0), (0, 0), (1, 1), (0, 0)))
    summed = jnp.zeros((padded.shape[0], frames, height, breadth, channels), jnp.float32)
    for time_tap in range(3):
        for row_tap in range(3):
            for col_tap in range(3):
                window = framed[
                    :,
                    time_tap : time_tap + frames,
                    row_tap : row_tap + height,
                    col_tap : col_tap + breadth,
                    :,
                ]
                summed = summed + window * kernel[9 * time_tap + 3 * row_tap + col_tap].astype(
                    jnp.float32
                )
    factor = lax.rsqrt(jnp.mean(summed * summed, axis=-1, keepdims=True) + 1e-05)
    normed = (summed * factor * gains.astype(jnp.float32)).astype(jnp.bfloat16)
    projected = jnp.dot(
        normed.reshape(-1, channels), weight, preferred_element_type=jnp.float32
    ).reshape(summed.shape)
    centre = padded[:, :, 1:-1].astype(jnp.float32)
    return (centre + jax.nn.gelu(projected)).astype(jnp.bfloat16)


def body(
    tiles,
    patch_index,
    pos_table,
    depth_kernel,
    enc_gain,
    point_weight,
    action_ids,
    w_in,
    action_table,
    dyn_gain,
    w_query,
    w_keyval,
    seq_order,
):
    frames = tiles.shape[1]
    height = tiles.shape[2]
    breadth = tiles.shape[3]
    channels = tiles.shape[4]
    positions = pos_table.shape[0]
    blocks = depth_kernel.shape[0]
    flat_index = patch_index.reshape(-1)
    position_pick = (flat_index[:, None] == jnp.arange(positions, dtype=jnp.int32)[None, :]).astype(
        jnp.bfloat16
    )
    placed = jnp.dot(position_pick, pos_table, preferred_element_type=jnp.float32).reshape(
        tiles.shape
    )
    hidden = (tiles.astype(jnp.float32) + placed).astype(jnp.bfloat16)
    for block_idx in range(blocks):
        padded = extended(hidden, (("seq", 2),), 1)
        hidden = depth_block(
            padded, depth_kernel[block_idx], enc_gain[block_idx], point_weight[block_idx]
        )
    latent = hidden.reshape(-1, channels)
    clips = action_ids.shape[0]
    actions = action_table.shape[0]
    cells = height * breadth
    action_range = jnp.arange(actions, dtype=jnp.int32)
    gathered = lax.all_gather(latent, "dp", axis=0, tiled=True)
    w_slab = lax.all_gather(w_in, "seq", axis=0, tiled=True)
    action_pick = (action_ids.reshape(-1)[:, None] == action_range[None, :]).astype(jnp.bfloat16)
    action_rows = jnp.dot(action_pick, action_table, preferred_element_type=jnp.float32)
    embed = jnp.dot(gathered, w_slab, preferred_element_type=jnp.float32).reshape(
        clips * frames, cells, -1
    )
    embed = jax.nn.gelu(embed + action_rows[:, None, :])
    squares = lax.psum(jnp.sum(embed * embed, axis=-1), "dp")
    factor = lax.rsqrt(squares / DIM + 1e-05)[:, :, None]
    normed = (
        (embed * factor * dyn_gain.astype(jnp.float32))
        .astype(jnp.bfloat16)
        .reshape(clips * frames * cells, -1)
    )
    inputs = lax.all_gather(normed, "dp", axis=1, tiled=True)
    pieces = (
        lax.all_gather(w_query, "seq", axis=0, tiled=True),
        lax.all_gather(w_keyval, "seq", axis=0, tiled=True),
    )
    span_rows = pieces[0].shape[0]
    query_sum = jnp.dot(inputs, pieces[0], preferred_element_type=jnp.float32)
    pair_sum = jnp.dot(inputs, pieces[1].reshape(span_rows, -1), preferred_element_type=jnp.float32)
    kv_local = w_keyval.shape[2] // HEAD
    group = Q_HEADS // KV_HEADS
    query_heads = query_sum.reshape(clips, frames, cells, kv_local, group, HEAD)
    pairs = pair_sum.reshape(clips, frames, cells, 2, kv_local, HEAD)
    key_heads = pairs[:, :, :, 0]
    value_heads = pairs[:, :, :, 1].astype(jnp.bfloat16)
    query_unit = query_heads * lax.rsqrt(
        jnp.mean(query_heads * query_heads, axis=-1, keepdims=True) + 1e-06
    )
    key_unit = key_heads * lax.rsqrt(
        jnp.mean(key_heads * key_heads, axis=-1, keepdims=True) + 1e-06
    )
    scores = jnp.einsum(
        "cfpkgh,ctpkh->cpkgft", query_unit, key_unit, precision=lax.Precision.HIGHEST
    ) * HEAD ** (-0.5)
    causal = (
        jnp.arange(frames, dtype=jnp.int32)[:, None] >= jnp.arange(frames, dtype=jnp.int32)[None, :]
    )
    raised = jnp.where(causal, jnp.exp(scores), 0.0)
    shares = (raised / jnp.sum(raised, axis=-1, keepdims=True)).astype(jnp.bfloat16)
    mixed = jnp.einsum(
        "cpkgft,ctpkh->cfpkgh", shares, value_heads, preferred_element_type=jnp.float32
    ).astype(jnp.bfloat16)
    mixed = mixed.reshape(clips, frames, height, breadth, -1)
    return jnp.take(mixed, seq_order, axis=3)


def solution(mesh):
    placed = (
        P("dp", None, "seq", None, None),
        P("dp", None, "seq", None),
        P(),
        P(),
        P(),
        P(),
        P(),
        P("seq", "dp"),
        P(None, "dp"),
        P("dp"),
        P("seq", "dp"),
        P("seq", None, "dp"),
        P(),
    )
    return jax.shard_map(
        body,
        mesh=mesh,
        in_specs=placed,
        out_specs=P(None, None, "seq", None, "dp"),
        check_vma=False,
    )
```

profile of v0, /device:TPU:0, one launch (start us, length us, event | category | flops | bytes accessed | tf_op | source)
XLA Modules:
  0.0 375.4 jit_solution(16638443497301449434)
XLA Ops:
  6.6 0.7 all-gather.5.cloned.1.call-update
  7.3 0.7 all-gather.9.cloned.1.call-update
  8.1 0.8 copy.46
  8.9 0.1 eq.30
  9.0 0.3 fusion.139
  9.3 0.1 reshape.919
  9.4 0.2 add_convert_fusion
  9.6 0.1 fusion.148
  9.7 1.3 collective-permute-start.1
  11.0 3.0 collective-permute-start
  14.1 0.1 eq.34
  14.2 0.1 slice_convert_fusion.27
  14.3 1.0 fusion.141
  15.3 0.3 maximum_convert_fusion
  15.6 4.4 %multiply_reduce_fusion.4 = (f32[16,2,4]{2,1,0:T(2,128)S(1)}, f32[1,16,2,4,1024]{4,3,2,1,0:T(4,128)S(1)}) fusion(f32[1024]{0:T(1024)S(1)} %bitcast.139, f32[1024]{0:T(1024)S(1)} %bitcast.140, f32[1,16,4,4,1024]{4,3,2,1,0:T(4,128)S(1)} %maximum_convert_fusion, f32[1024]{0:T(1024)S(1)} %bitcast.141, f32[1024]{0:T(1024)S(1)} %bitcast.142, ...), kind=kLoop, calls=%fused_computation.212 | loop fusion | flops 7208832 | bytes 3256832 | tf_op jit(solution)/shard_map/reduce_sum | solution.py:45
  20.1 0.1 copy.47
  20.2 0.1 copy.48
  20.3 0.2 multiply_convert_fusion.2
  20.5 0.1 reshape.920
  20.6 2.1 fusion.12
  22.7 0.1 reshape.921
  22.9 0.4 fusion.136
  23.3 0.1 fusion.147
  23.4 1.3 collective-permute-start.3
  24.7 6.1 %collective-permute-start.2 = (bf16[1,16,1,4,1024]{4,3,2,1,0:T(4,128)(2,1)S(1)}, bf16[1,16,1,4,1024]{4,3,2,1,0:T(4,128)(2,1)S(1)}, u32[]{:S(2)}, u32[]{:S(2)}) collective-permute-start(bf16[1,16,1,4,1024]{4,3,2,1,0:T(4,128)(2,1)S(1)} %get-tuple-element.9), channel_id=1, source_target_pairs={{0,1},{1,2},{2,3},{3,4},{4,5},{5,6},{6,7},{7,8},{8,9},{9,10},{10,1... | collective-permute-start | bytes 393224 | tf_op jit(solution)/shard_map/ppermute | solution.py:17
  30.8 0.1 slice_convert_fusion.28
  30.9 0.9 collective-permute-done.2
  31.8 0.3 maximum_convert_fusion.1
  32.1 4.4 %multiply_reduce_fusion.3 = (f32[16,2,4]{2,1,0:T(2,128)S(1)}, f32[1,16,2,4,1024]{4,3,2,1,0:T(4,128)S(1)}) fusion(f32[1024]{0:T(1024)S(1)} %bitcast.117, f32[1024]{0:T(1024)S(1)} %bitcast.118, f32[1,16,4,4,1024]{4,3,2,1,0:T(4,128)S(1)} %maximum_convert_fusion.1, f32[1024]{0:T(1024)S(1)} %bitcast.153, f32[1024]{0:T(1024)S(1)} %bitcast.154, ...), kind=kLoop, calls=%fused_computation.210 | loop fusion | flops 7208832 | bytes 3256832 | tf_op jit(solution)/shard_map/reduce_sum | solution.py:45
  36.5 0.1 copy.49
  36.6 0.1 copy.50
  36.7 0.2 multiply_convert_fusion.1
  36.9 0.1 reshape.922
  37.0 2.1 fusion.10
  39.1 0.1 reshape.923
  39.2 0.4 fusion.135
  39.6 0.1 reshape.924
  39.7 7.0 %all_gather.15 = bf16[256,1024]{1,0:T(8,128)(2,1)S(1)} all-gather(bf16[128,1024]{1,0:T(8,128)(2,1)S(1)} %reshape.924), channel_id=1, replica_groups=mesh['dp'=2,'seq'=16] {'dp'}, dimensions={0}, use_global_device_ids=true | all-gather | bytes 786432 | tf_op jit(solution)/shard_map/all_gather | solution.py:93
  46.8 21.4 %all-gather.5.cloned.1.call-done = bf16[1024,2560]{1,0:T(8,128)(2,1)} async-done(((bf16[64,2560]{1,0:T(8,128)(2,1)}), bf16[1024,2560]{1,0:T(8,128)(2,1)}) %all-gather.5.cloned.1.call-update) | async-done | bytes 5242896 | tf_op jit(solution)/shard_map/all_gather | solution.py:94
  68.2 4.6 %multiply_reduce_fusion.1 = (f32[256]{0:T(256)S(1)}, f32[256,2560]{1,0:T(8,128)S(1)}) fusion(f32[32,2560]{1,0:T(8,128)} %fusion.141, bf16[256,1024]{1,0:T(8,128)(2,1)S(1)} %all_gather.15, bf16[1024,2560]{1,0:T(8,128)(2,1)} %all-gather.5.cloned.1.call-done), kind=kOutput, calls=%fused_computation.64 | convolution fusion | flops 1349385984 | bytes 8717312 | tf_op jit(solution)/shard_map/dot_general | solution.py:97
  72.8 0.1 reduce_sum.59
  72.8 8.1 %psum.7 = f32[32,8]{1,0:T(8,128)S(1)} all-reduce(f32[32,8]{1,0:T(8,128)S(1)} %reduce_sum.59), channel_id=1, replica_groups=mesh['dp'=2,'seq'=16] {'dp'}, use_global_device_ids=true, to_apply=%region_3.4 | all-reduce | flops 256 | bytes 2048 | tf_op jit(solution)/shard_map/psum | solution.py:101
  81.0 0.1 mul.774
  81.1 1.3 multiply_convert_fusion
  82.4 0.2 all-gather.11.cloned.1.call-start
  82.7 0.3 all-gather.11.cloned.1.call-update
  83.1 73.5 %all-gather.9.cloned.1.call-done = bf16[5120,2,512]{2,1,0:T(2,128)(2,1)} async-done(((bf16[320,2,512]{2,1,0:T(2,128)(2,1)}), bf16[5120,2,512]{2,1,0:T(2,128)(2,1)}) %all-gather.9.cloned.1.call-update) | async-done | bytes 10485776 | tf_op jit(solution)/shard_map/all_gather | solution.py:111
  156.6 26.3 %copy.63 = bf16[5120,2,512]{0,2,1:T(8,128)(2,1)} copy(bf16[5120,2,512]{2,1,0:T(2,128)(2,1)} %all-gather.9.cloned.1.call-done) | data formatting | bytes 20971520 | tf_op jit(solution)/shard_map/reshape | solution.py:115
  182.9 12.5 %all-gather.7.cloned.1.call-done = bf16[256,5120]{1,0:T(8,128)(2,1)} async-done(((bf16[256,2560]{1,0:T(8,128)(2,1)}), bf16[256,5120]{1,0:T(8,128)(2,1)}) %all-gather.7.cloned.1.call-update) | async-done | bytes 2621456 | tf_op jit(solution)/shard_map/all_gather | solution.py:108
  195.4 6.5 %fusion.149 = f32[2,16,8,2,4,128]{5,2,4,3,1,0:T(8,128)S(1)} fusion(bf16[2,16,8,5120,1,1]{3,2,5,4,1,0:T(8,128)(2,1)} %bitcast.173, bf16[2,4,128,5120,1,1]{3,2,1,0,5,4:T(8,128)(2,1)} %bitcast.114), kind=kOutput, calls=%fused_computation.292 | convolution fusion | flops 2684354560 | bytes 14155776 | tf_op jit(solution)/shard_map/dot_general | solution.py:115
  201.9 0.3 multiply_reduce_fusion.2
  202.2 0.2 multiply_bitcast_fusion
  202.4 127.9 %all-gather.11.cloned.1.call-done = bf16[5120,2560]{1,0:T(8,128)(2,1)} async-done(((bf16[320,2560]{1,0:T(8,128)(2,1)}), bf16[5120,2560]{1,0:T(8,128)(2,1)}) %all-gather.11.cloned.1.call-update) | async-done | bytes 26214416 | tf_op jit(solution)/shard_map/all_gather | solution.py:110
  330.4 12.8 %fusion.150 = f32[256,2560]{1,0:T(8,128)S(1)} fusion(bf16[256,5120]{1,0:T(8,128)(2,1)} %all-gather.7.cloned.1.call-done, bf16[5120,2560]{1,0:T(8,128)(2,1)} %all-gather.11.cloned.1.call-done), kind=kOutput, calls=%fused_computation.293 | convolution fusion | flops 6710886400 | bytes 31457280 | tf_op jit(solution)/shard_map/dot_general | solution.py:114
  343.1 0.7 multiply_reduce_fusion
  343.9 0.1 add_rsqrt_fusion
  344.0 0.8 broadcast_multiply_fusion
  344.8 15.7 %fusion.9 = (f32[2,8,4,5,16]{4,3,2,1,0:T(8,128)S(1)}, f32[2,8,4,16,16,5]{4,3,5,2,1,0:T(8,128)S(1)}) fusion(pred[16,16]{0,1:T(8,128)(4,1)S(1)} %iota_compare_fusion.4, f32[2,16,8,4,5,128]{5,2,4,3,1,0:T(8,128)S(1)} %broadcast_multiply_fusion, f32[2,16,8,4,128,1]{4,2,3,1,0,5:T(8,128)S(1)} %multiply_bitcast_fusion), kind=kOutput, calls=%fused_computation.65 | convolution fusion | flops 126069760 | bytes 3494144 | tf_op jit(solution)/shard_map/cfpkgh,ctpkh->cpkgft/dot_general | solution.py:128
  360.5 1.2 fusion.16
  361.7 0.5 copy.56
  362.3 2.3 reshape.927
  364.6 2.0 gather_fusion
  366.6 0.2 select_bitcast_fusion
  366.8 2.1 copy.57
  (37 shorter events, 0.4 us)
Async XLA Ops:
  6.5 2.5 copy-start
  6.5 2.9 copy-start.3
  6.5 7.5 %copy-start.7 = (s32[2,16]{1,0:T(2,128)S(1)}, s32[2,16]{1,0:T(2,128)}, u32[]{:S(2)}) copy-start(s32[2,16]{1,0:T(2,128)} %param.19) | copy-start | bytes 388
  6.5 7.6 %copy-start.6 = (bf16[2560]{0:T(1024)(128)(2,1)S(1)}, bf16[2560]{0:T(1024)(128)(2,1)}, u32[]{:S(2)}) copy-start(bf16[2560]{0:T(1024)(128)(2,1)} %param.22) | copy-start | bytes 15364
  6.5 7.6 %copy-start.2 = (bf16[2,27,1024]{2,0,1:T(2,128)(2,1)S(1)}, bf16[2,27,1024]{2,0,1:T(2,128)(2,1)}, u32[]{:S(2)}) copy-start(bf16[2,27,1024]{2,0,1:T(2,128)(2,1)} %param.16) | copy-start | bytes 331780
  6.5 7.7 %copy-start.4 = (bf16[8,2560]{1,0:T(8,128)(2,1)S(1)}, bf16[8,2560]{1,0:T(8,128)(2,1)}, u32[]{:S(2)}) copy-start(bf16[8,2560]{1,0:T(8,128)(2,1)} %param.21) | copy-start | bytes 122884
  6.6 8.7 %copy-start.5 = (bf16[2,1024]{1,0:T(2,128)(2,1)S(1)}, bf16[2,1024]{1,0:T(2,128)(2,1)}, u32[]{:S(2)}) copy-start(bf16[2,1024]{1,0:T(2,128)(2,1)} %param.17) | copy-start | bytes 12292
  6.6 61.6 %all-gather.5.cloned.1.call-start = ((), (), s32[]{:S(2)}) async-start(), calls=%async_computation | async-start | bytes 5570560 | tf_op jit(solution)/shard_map/all_gather | solution.py:94
  7.3 149.3 %all-gather.9.cloned.1.call-start = ((), (), s32[]{:S(2)}) async-start(), calls=%async_computation.2 | async-start | bytes 11141120 | tf_op jit(solution)/shard_map/all_gather | solution.py:111
  8.1 187.4 %all-gather.7.cloned.1.call-start = ((), (), s32[]{:S(2)}) async-start(), calls=%async_computation.1 | async-start | bytes 3932160 | tf_op jit(solution)/shard_map/all_gather | solution.py:108
  9.7 5.6 %collective-permute-start.1 = (bf16[1,16,1,4,1024]{4,3,2,1,0:T(4,128)(2,1)S(1)}, bf16[1,16,1,4,1024]{4,3,2,1,0:T(4,128)(2,1)S(1)}, u32[]{:S(2)}, u32[]{:S(2)}) collective-permute-start(bf16[1,16,1,4,1024]{4,3,2,1,0:T(4,128)(2,1)S(1)} %get-tuple-element.12), channel_id=1, source_target_pairs={{1,0},{2,1},{3,2},{4,3},{5,4},{6,5},{7,6},{8,7},{9,8},{10,9},{11,1... | collective-permute-start | bytes 393224 | tf_op jit(solution)/shard_map/ppermute | solution.py:20
  11.0 4.3 %collective-permute-start = (bf16[1,16,1,4,1024]{4,3,2,1,0:T(4,128)(2,1)S(1)}, bf16[1,16,1,4,1024]{4,3,2,1,0:T(4,128)(2,1)S(1)}, u32[]{:S(2)}, u32[]{:S(2)}) collective-permute-start(bf16[1,16,1,4,1024]{4,3,2,1,0:T(4,128)(2,1)S(1)} %get-tuple-element.11), channel_id=1, source_target_pairs={{0,1},{1,2},{2,3},{3,4},{4,5},{5,6},{6,7},{7,8},{8,9},{9,10},{10,1... | collective-permute-start | bytes 393224 | tf_op jit(solution)/shard_map/ppermute | solution.py:17
  23.4 7.5 %collective-permute-start.3 = (bf16[1,16,1,4,1024]{4,3,2,1,0:T(4,128)(2,1)S(1)}, bf16[1,16,1,4,1024]{4,3,2,1,0:T(4,128)(2,1)S(1)}, u32[]{:S(2)}, u32[]{:S(2)}) collective-permute-start(bf16[1,16,1,4,1024]{4,3,2,1,0:T(4,128)(2,1)S(1)} %get-tuple-element.10), channel_id=1, source_target_pairs={{1,0},{2,1},{3,2},{4,3},{5,4},{6,5},{7,6},{8,7},{9,8},{10,9},{11,1... | collective-permute-start | bytes 393224 | tf_op jit(solution)/shard_map/ppermute | solution.py:20
  24.7 7.1 %collective-permute-start.2 = (bf16[1,16,1,4,1024]{4,3,2,1,0:T(4,128)(2,1)S(1)}, bf16[1,16,1,4,1024]{4,3,2,1,0:T(4,128)(2,1)S(1)}, u32[]{:S(2)}, u32[]{:S(2)}) collective-permute-start(bf16[1,16,1,4,1024]{4,3,2,1,0:T(4,128)(2,1)S(1)} %get-tuple-element.9), channel_id=1, source_target_pairs={{0,1},{1,2},{2,3},{3,4},{4,5},{5,6},{6,7},{7,8},{8,9},{9,10},{10,1... | collective-permute-start | bytes 393224 | tf_op jit(solution)/shard_map/ppermute | solution.py:17
  81.1 2.0 copy-start.8
  82.4 247.9 %all-gather.11.cloned.1.call-start = ((), (), s32[]{:S(2)}) async-start(), calls=%async_computation.3 | async-start | bytes 27852800 | tf_op jit(solution)/shard_map/all_gather | solution.py:110
  364.6 4.3 %copy-start.1 = (bf16[128,1024]{1,0:T(8,128)(2,1)S(1)}, bf16[128,1024]{1,0:T(8,128)(2,1)}, u32[]{:S(2)}) copy-start(bf16[128,1024]{1,0:T(8,128)(2,1)} %param.15) | copy-start | bytes 786436
Sparse Core Ops, SparseCore 0:
  9.7 58.4 all-gather.4
  70.4 86.0 all-gather.8
  158.1 37.2 all-gather.6
  196.9 133.4 all-gather.10
where the time goes:
time: 376 us; the launch traced here: 375 us
  waiting for transfers between devices  238 us (63%)
  matrix products  46.1 us (12%)
  local copies, waits for them, and re-layouts  35.7 us (9%)
  blocking collectives  15.2 us (4%)
  other arithmetic  14.9 us (4%)
  between operations  13.5 us (4%)
  starting transfers between devices  12.1 us (3%)
    all_gather x1, waiting for transfers between devices, body(): lax.all_gather(w_query, 'seq', axis=0, tiled=True)  128 us
    all_gather x1, waiting for transfers between devices, body(): lax.all_gather(w_keyval, 'seq', axis=0, tiled=True)  73.5 us
    reshape x1, local copies, waits for them, and re-layouts, body(): pieces[1].reshape(span_rows, -1)  26.3 us
    all_gather x1, waiting for transfers between devices, body(): w_slab = lax.all_gather(w_in, 'seq', axis=0, tiled=True)  21.4 us
    dot_general x1, matrix products, body(): jnp.einsum('cfpkgh,ctpkh->cpkgft', query_unit, key_unit, precision=lax.Pr...  15.7 us
    dot_general x1, matrix products, body(): query_sum = jnp.dot(inputs, pieces[0], preferred_element_type=jnp.float32)  12.8 us
    all_gather x1, waiting for transfers between devices, body(): inputs = lax.all_gather(normed, 'dp', axis=1, tiled=True)  12.5 us
    ppermute x2, starting transfers between devices, extended(): lax.ppermute(lax.slice_in_dim(block, block.shape[dim] - width, None, axis...  9.14 us
  transfers between devices with their start and end apart: 8, of which 5 were waited for; matrix products, arithmetic and copies ran while one was open for 16% of the time, Pallas kernels for 0%

commit v1 on v0

--- a/solution.py
+++ b/solution.py
@@ -7,6 +7,18 @@
 HEAD = 128
 Q_HEADS = 40
 KV_HEADS = 8
+
+
+def plane_unite(x_in):
+    return jnp.concatenate(
+        lax.all_to_all(
+            jnp.stack([x_in for _ in range(lax.axis_size("seq"))]),
+            concat_axis=0,
+            axis_name="seq",
+            split_axis=0,
+        ),
+        0,
+    )
 
 
 def extended(block, sides, width):
@@ -106,10 +118,7 @@
         .reshape(clips * frames * cells, -1)
     )
     inputs = lax.all_gather(normed, "dp", axis=1, tiled=True)
-    pieces = (
-        lax.all_gather(w_query, "seq", axis=0, tiled=True),
-        lax.all_gather(w_keyval, "seq", axis=0, tiled=True),
-    )
+    pieces = (lax.all_gather(w_query, "seq", axis=0, tiled=True), plane_unite(w_keyval))
     span_rows = pieces[0].shape[0]
     query_sum = jnp.dot(inputs, pieces[0], preferred_element_type=jnp.float32)
     pair_sum = jnp.dot(inputs, pieces[1].reshape(span_rows, -1), preferred_element_type=jnp.float32)

time: 376 us -> 523 us (1.39)
  the two profiles are of different devices: /device:TPU:0 before, /device:TPU:13 now
where the time goes in v1:
time: 523 us; the launch traced here: 514 us
  waiting for transfers between devices  358 us (68%)
  matrix products  46 us (9%)
  local copies, waits for them, and re-layouts  43.9 us (8%)
  starting transfers between devices  22.3 us (4%)
  other arithmetic  16.1 us (3%)
  between operations  13.7 us (3%)
  blocking collectives  13.5 us (3%)
    all_to_all x1, waiting for transfers between devices, plane_unite(): lax.all_to_all(jnp.stack([x_in for _ in range(lax.axis_size('seq'))]), co...  339 us
    dot_general x1, matrix products, body(): jnp.einsum('cfpkgh,ctpkh->cpkgft', query_unit, key_unit, precision=lax.Pr...  15.7 us
    all_gather x1, waiting for transfers between devices, body(): w_slab = lax.all_gather(w_in, 'seq', axis=0, tiled=True)  15.3 us
    dot_general x1, local copies, waits for them, and re-layouts, body(): jnp.dot(inputs, pieces[1].reshape(span_rows, -1), preferred_element_type=...  13.9 us
    dot_general x1, matrix products, body(): query_sum = jnp.dot(inputs, pieces[0], preferred_element_type=jnp.float32)  12.8 us
    unnamed x20, local copies, waits for them, and re-layouts  12.2 us
  transfers between devices with their start and end apart: 8, of which 5 were waited for; matrix products, arithmetic and copies ran while one was open for 12% of the time, Pallas kernels for 0%

profile of v1, /device:TPU:13, one launch (start us, length us, event | category | flops | bytes accessed | tf_op | source)
XLA Modules:
  0.0 513.6 jit_solution(1115510435195503946)
XLA Ops:
  6.6 0.7 all-gather.4.cloned.1.call-update
  7.3 0.8 copy.46
  8.1 0.1 eq.30
  8.2 0.3 fusion.139
  8.5 0.1 reshape.918
  8.7 1.1 add_convert_fusion
  9.8 0.1 fusion.148
  9.9 2.6 collective-permute-start.1
  12.5 3.9 collective-permute-start
  16.4 0.1 eq.34
  16.5 0.1 slice_convert_fusion.27
  16.6 1.0 fusion.141
  17.6 0.7 collective-permute-done
  18.3 0.3 maximum_convert_fusion
  18.6 4.4 multiply_reduce_fusion.4
  23.1 0.1 copy.47
  23.2 0.1 copy.48
  23.3 0.2 multiply_convert_fusion.2
  23.5 2.0 fusion.12
  25.6 0.1 reshape.920
  25.7 0.4 fusion.136
  26.2 0.1 fusion.147
  26.3 2.8 collective-permute-start.3
  29.1 4.4 collective-permute-start.2
  33.5 0.1 slice_convert_fusion.28
  33.5 1.1 collective-permute-done.3
  34.6 0.7 collective-permute-done.2
  35.4 0.3 maximum_convert_fusion.1
  35.7 4.4 multiply_reduce_fusion.3
  40.2 0.1 copy.49
  40.3 0.1 copy.50
  40.4 0.2 multiply_convert_fusion.1
  40.6 0.1 reshape.921
  40.6 2.0 fusion.10
  42.7 0.1 reshape.922
  42.8 0.4 fusion.135
  43.3 7.4 %all_gather.12 = bf16[256,1024]{1,0:T(8,128)(2,1)S(1)} all-gather(bf16[128,1024]{1,0:T(8,128)(2,1)S(1)} %reshape.923), channel_id=1, replica_groups=mesh['dp'=2,'seq'=16] {'dp'}, dimensions={0}, use_global_device_ids=true | all-gather | bytes 786432 | tf_op jit(solution)/shard_map/all_gather | solution.py:105
  50.7 15.3 %all-gather.4.cloned.1.call-done = bf16[1024,2560]{1,0:T(8,128)(2,1)} async-done(((bf16[64,2560]{1,0:T(8,128)(2,1)}), bf16[1024,2560]{1,0:T(8,128)(2,1)}) %all-gather.4.cloned.1.call-update) | async-done | bytes 5242896 | tf_op jit(solution)/shard_map/all_gather | solution.py:106
  66.0 4.6 multiply_reduce_fusion.1
  70.6 0.1 reduce_sum.59
  70.7 6.1 %psum.7 = f32[32,8]{1,0:T(8,128)S(1)} all-reduce(f32[32,8]{1,0:T(8,128)S(1)} %reduce_sum.59), channel_id=1, replica_groups=mesh['dp'=2,'seq'=16] {'dp'}, use_global_device_ids=true, to_apply=%region_3.4 | all-reduce | flops 256 | bytes 2048 | tf_op jit(solution)/shard_map/psum | solution.py:113
  76.8 0.1 mul.774
  77.0 1.3 multiply_convert_fusion
  78.3 0.5 all-gather.8.cloned.1.call-start
  78.8 0.2 all-gather.8.cloned.1.call-update
  79.1 9.3 %stack.2 = bf16[16,320,2,512]{3,2,1,0:T(2,128)(2,1)} broadcast(bf16[320,2,512]{2,1,0:T(2,128)(2,1)S(1)} %copy-done.2), dimensions={1,2,3} | broadcast | bytes 11141120 | tf_op jit(solution)/shard_map/stack | solution.py:15
  88.4 8.0 %all-to-all-start = ((bf16[16,320,2,512]{3,2,1,0:T(2,128)(2,1)}), bf16[16,320,2,512]{3,2,1,0:T(2,128)(2,1)}, u32[]{:S(2)}, u32[]{:S(2)}) async-start(bf16[16,320,2,512]{3,2,1,0:T(2,128)(2,1)} %stack.2), calls=%async_computation | async-start | bytes 20971520 | tf_op jit(solution)/shard_map/all_to_all | solution.py:14
  96.5 339.4 %all-to-all-done = bf16[16,320,2,512]{3,2,1,0:T(2,128)(2,1)} async-done(((bf16[16,320,2,512]{3,2,1,0:T(2,128)(2,1)}), bf16[16,320,2,512]{3,2,1,0:T(2,128)(2,1)}, u32[]{:S(2)}, u32[]{:S(2)}) %all-to-all-start) | async-done | bytes 10485792 | tf_op jit(solution)/shard_map/all_to_all | solution.py:14
  435.8 11.4 %copy.67 = bf16[640,8,2,512]{3,1,2,0:T(8,128)(2,1)} copy(bf16[640,8,2,512]{3,2,1,0:T(2,128)(2,1)} %bitcast.80) | data formatting | bytes 20971520
  447.2 13.9 %copy.51 = bf16[1024,5120]{1,0:T(8,128)(2,1)} copy(bf16[1024,5120]{0,1:T(8,128)(2,1)} %bitcast.115) | data formatting | bytes 20971520 | tf_op jit(solution)/shard_map/dot_general | solution.py:124
  461.1 6.5 %fusion.149 = f32[2,16,8,2,4,128]{5,2,4,3,1,0:T(8,128)S(1)} fusion(bf16[2,16,8,5120,1,1]{3,2,5,4,1,0:T(8,128)(2,1)} %bitcast.175, bf16[2,4,128,5120,1,1]{3,2,1,0,5,4:T(8,128)(2,1)} %bitcast.116), kind=kOutput, calls=%fused_computation.292 | convolution fusion | flops 2684354560 | bytes 14155776 | tf_op jit(solution)/shard_map/dot_general | solution.py:124
  467.6 0.3 multiply_reduce_fusion.2
  467.9 0.2 multiply_bitcast_fusion
  468.1 12.8 %fusion.150 = f32[256,2560]{1,0:T(8,128)S(1)} fusion(bf16[256,5120]{1,0:T(8,128)(2,1)} %all-gather.6.cloned.1.call-done, bf16[5120,2560]{1,0:T(8,128)(2,1)} %all-gather.8.cloned.1.call-done), kind=kOutput, calls=%fused_computation.293 | convolution fusion | flops 6710886400 | bytes 31457280 | tf_op jit(solution)/shard_map/dot_general | solution.py:123
  480.9 0.7 multiply_reduce_fusion
  481.7 0.1 add_rsqrt_fusion
  481.8 1.1 broadcast_multiply_fusion
  482.8 15.7 %fusion.9 = (f32[2,8,4,5,16]{4,3,2,1,0:T(8,128)S(1)}, f32[2,8,4,16,16,5]{4,3,5,2,1,0:T(8,128)S(1)}) fusion(pred[16,16]{0,1:T(8,128)(4,1)S(1)} %iota_compare_fusion.4, f32[2,16,8,4,5,128]{5,2,4,3,1,0:T(8,128)S(1)} %broadcast_multiply_fusion, f32[2,16,8,4,128,1]{4,2,3,1,0,5:T(8,128)S(1)} %multiply_bitcast_fusion), kind=kOutput, calls=%fused_computation.65 | convolution fusion | flops 126069760 | bytes 3494144 | tf_op jit(solution)/shard_map/cfpkgh,ctpkh->cpkgft/dot_general | solution.py:137
  498.6 1.2 fusion.16
  499.7 0.5 copy.56
  500.3 2.3 reshape.925
  502.6 2.0 gather_fusion
  504.6 0.2 select_bitcast_fusion
  504.8 2.1 copy.57
  (38 shorter events, 0.5 us)
Async XLA Ops:
  6.5 1.7 copy-start
  6.5 9.8 %copy-start.7 = (s32[2,16]{1,0:T(2,128)S(1)}, s32[2,16]{1,0:T(2,128)}, u32[]{:S(2)}) copy-start(s32[2,16]{1,0:T(2,128)} %param.19) | copy-start | bytes 388
  6.5 9.9 %copy-start.6 = (bf16[2560]{0:T(1024)(128)(2,1)S(1)}, bf16[2560]{0:T(1024)(128)(2,1)}, u32[]{:S(2)}) copy-start(bf16[2560]{0:T(1024)(128)(2,1)} %param.22) | copy-start | bytes 15364
  6.5 9.9 %copy-start.3 = (bf16[2,27,1024]{2,0,1:T(2,128)(2,1)S(1)}, bf16[2,27,1024]{2,0,1:T(2,128)(2,1)}, u32[]{:S(2)}) copy-start(bf16[2,27,1024]{2,0,1:T(2,128)(2,1)} %param.16) | copy-start | bytes 331780
  6.5 10.1 %copy-start.4 = (bf16[8,2560]{1,0:T(8,128)(2,1)S(1)}, bf16[8,2560]{1,0:T(8,128)(2,1)}, u32[]{:S(2)}) copy-start(bf16[8,2560]{1,0:T(8,128)(2,1)} %param.21) | copy-start | bytes 122884
  6.5 11.0 %copy-start.5 = (bf16[2,1024]{1,0:T(2,128)(2,1)S(1)}, bf16[2,1024]{1,0:T(2,128)(2,1)}, u32[]{:S(2)}) copy-start(bf16[2,1024]{1,0:T(2,128)(2,1)} %param.17) | copy-start | bytes 12292
  6.6 59.5 %all-gather.4.cloned.1.call-start = ((), (), s32[]{:S(2)}) async-start(), calls=%async_computation.1 | async-start | bytes 5570560 | tf_op jit(solution)/shard_map/all_gather | solution.py:106
  7.3 453.8 %all-gather.6.cloned.1.call-start = ((), (), s32[]{:S(2)}) async-start(), calls=%async_computation.2 | async-start | bytes 3932160 | tf_op jit(solution)/shard_map/all_gather | solution.py:120
  9.9 7.7 %collective-permute-start.1 = (bf16[1,16,1,4,1024]{4,3,2,1,0:T(4,128)(2,1)S(1)}, bf16[1,16,1,4,1024]{4,3,2,1,0:T(4,128)(2,1)S(1)}, u32[]{:S(2)}, u32[]{:S(2)}) collective-permute-start(bf16[1,16,1,4,1024]{4,3,2,1,0:T(4,128)(2,1)S(1)} %get-tuple-element.12), channel_id=1, source_target_pairs={{1,0},{2,1},{3,2},{4,3},{5,4},{6,5},{7,6},{8,7},{9,8},{10,9},{11,1... | collective-permute-start | bytes 393224 | tf_op jit(solution)/shard_map/ppermute | solution.py:32
  12.5 5.8 %collective-permute-start = (bf16[1,16,1,4,1024]{4,3,2,1,0:T(4,128)(2,1)S(1)}, bf16[1,16,1,4,1024]{4,3,2,1,0:T(4,128)(2,1)S(1)}, u32[]{:S(2)}, u32[]{:S(2)}) collective-permute-start(bf16[1,16,1,4,1024]{4,3,2,1,0:T(4,128)(2,1)S(1)} %get-tuple-element.11), channel_id=1, source_target_pairs={{0,1},{1,2},{2,3},{3,4},{4,5},{5,6},{6,7},{7,8},{8,9},{9,10},{10,1... | collective-permute-start | bytes 393224 | tf_op jit(solution)/shard_map/ppermute | solution.py:29
  26.3 8.4 %collective-permute-start.3 = (bf16[1,16,1,4,1024]{4,3,2,1,0:T(4,128)(2,1)S(1)}, bf16[1,16,1,4,1024]{4,3,2,1,0:T(4,128)(2,1)S(1)}, u32[]{:S(2)}, u32[]{:S(2)}) collective-permute-start(bf16[1,16,1,4,1024]{4,3,2,1,0:T(4,128)(2,1)S(1)} %get-tuple-element.10), channel_id=1, source_target_pairs={{1,0},{2,1},{3,2},{4,3},{5,4},{6,5},{7,6},{8,7},{9,8},{10,9},{11,1... | collective-permute-start | bytes 393224 | tf_op jit(solution)/shard_map/ppermute | solution.py:32
  29.1 6.3 %collective-permute-start.2 = (bf16[1,16,1,4,1024]{4,3,2,1,0:T(4,128)(2,1)S(1)}, bf16[1,16,1,4,1024]{4,3,2,1,0:T(4,128)(2,1)S(1)}, u32[]{:S(2)}, u32[]{:S(2)}) collective-permute-start(bf16[1,16,1,4,1024]{4,3,2,1,0:T(4,128)(2,1)S(1)} %get-tuple-element.9), channel_id=1, source_target_pairs={{0,1},{1,2},{2,3},{3,4},{4,5},{5,6},{6,7},{7,8},{8,9},{9,10},{10,1... | collective-permute-start | bytes 393224 | tf_op jit(solution)/shard_map/ppermute | solution.py:29
  76.9 2.1 copy-start.2
  78.3 389.8 %all-gather.8.cloned.1.call-start = ((), (), s32[]{:S(2)}) async-start(), calls=%async_computation.3 | async-start | bytes 27852800 | tf_op jit(solution)/shard_map/all_gather | solution.py:121
  88.4 8.1 %copy-start.8 = (s32[4]{0:T(128)S(1)}, s32[4]{0:T(128)}, u32[]{:S(2)}) copy-start(s32[4]{0:T(128)} %param.25) | copy-start | bytes 52
  88.4 347.4 %all-to-all-start = ((bf16[16,320,2,512]{3,2,1,0:T(2,128)(2,1)}), bf16[16,320,2,512]{3,2,1,0:T(2,128)(2,1)}, u32[]{:S(2)}, u32[]{:S(2)}) async-start(bf16[16,320,2,512]{3,2,1,0:T(2,128)(2,1)} %stack.2), calls=%async_computation | async-start | bytes 20971520 | tf_op jit(solution)/shard_map/all_to_all | solution.py:14
  502.6 4.3 copy-start.1
Sparse Core Ops, SparseCore 0:
  9.6 56.3 all-gather.3
  78.4 39.0 all-gather.5
  119.1 329.4 all-gather.7
